TPU v7x, 32 devices: a whole 2x2x4 slice. The times are simulated.
32 devices in a mesh: group: 4 (over y, core), peer: 8 (over z, x).
Axes of the slice: x: 2, y: 2, z: 4, core: 2. Of those that a mesh axis runs over, the one named last changes fastest.
Arguments:
- states: float32 [41, 1048576], P(None, ('group', 'peer')), may hold values from -6 to 6
- block_part: int32 [8192], P(('group', 'peer')), may hold values from 0 to 31, as said below
- tile_perm: int32 [8192, 128], P(('group', 'peer')), may hold values from 0 to 127, each once within a row
- half_volt: float32 [40], replicated, may hold values from -4 to 4
- steepness: float32 [40], replicated, may hold values from 0.5 to 4
- gate_rate: float32 [40], replicated, may hold values from 0.1 to 1
- conductance: float32 [40], replicated, may hold values from 0.005 to 0.08
- reversal: float32 [40], replicated, may hold values from -6 to 6
Outputs:
- regrouped: float32 [41, 1048576], P(None, ('group', 'peer'))
Inputs may be any that keep to these rules, and one draw needn't show every extreme that they name: `block_part`: every partition holds exactly 256 blocks. Within each slab of 256 consecutive global blocks no partition holds more than 16 blocks; every slab has exactly 16 blocks of some partition, and every partition has exactly 16 blocks in some slab.
All inputs are finite; a program needn't handle non-finite values.
Results may differ from a plain program's by a relative error of at most 0.0001.
Values sent between devices are 32-bit elements; how exact they have to be, the bound alone decides.
No kernel may reach another device: no remote copies, remote signals or barrier semaphores. Data moves between devices by JAX's collectives and lax.ppermute only.
A program may use at most 192 MiB of HBM per device.

v0:
```python
import jax
import jax.numpy as jnp
from jax import lax
from jax.sharding import PartitionSpec as P

time_step = 0.25


def entering(part, axis, combine, identity):
    place = lax.axis_index(axis)
    gathered = lax.all_gather(part, axis)
    state = jnp.zeros_like(part) + jnp.asarray(identity, part.dtype)

    def one(step, state):
        return combine(state, lax.dynamic_index_in_dim(gathered, step, 0, False))

    return lax.fori_loop(0, place, one, state)


def advance(state_rows, half_volt, steepness, gate_rate, conductance, reversal):
    voltage = state_rows[0:1]
    gate_vals = state_rows[1:]
    steady = jax.nn.sigmoid((voltage - half_volt[:, None]) * steepness[:, None])
    damping = jnp.exp(-gate_rate[:, None] * (1.0 + jax.nn.sigmoid(voltage)))
    gate_vals = steady + (gate_vals - steady) * damping
    current = jnp.sum(
        conductance[:, None] * gate_vals * (voltage - reversal[:, None]), axis=0, keepdims=True
    )
    voltage = voltage - time_step * current
    return jnp.concatenate([voltage, gate_vals], axis=0)


def add_counts(earlier, later):
    return earlier + later


def on_device(
    states, block_part, tile_perm, half_volt, steepness, gate_rate, conductance, reversal
):
    devices = lax.axis_size(("group", "peer"))
    local_blocks = block_part.shape[0]
    tile_width = tile_perm.shape[1]
    width = states.shape[0]
    capacity = 2 * local_blocks // devices
    partitions = jnp.arange(devices, dtype=jnp.int32)
    onehot = (block_part[:, None] == partitions[None, :]).astype(jnp.int32)
    counts = jnp.sum(onehot, axis=0, dtype=jnp.int32)
    earlier = entering(counts, ("group", "peer"), add_counts, jnp.zeros_like(counts))
    rank_in = jnp.sum(
        (jnp.cumsum(onehot, axis=0, dtype=jnp.int32) - onehot) * onehot, axis=1, dtype=jnp.int32
    )
    local_index = jnp.sum(onehot * earlier[None, :], axis=1, dtype=jnp.int32) + rank_in
    slot_index = block_part * capacity + rank_in
    requests = jnp.full((devices * capacity,), -1, jnp.int32).at[slot_index].set(local_index)
    requests = requests.reshape(devices, capacity)
    advanced = advance(states, half_volt, steepness, gate_rate, conductance, reversal)
    advanced = advanced.reshape(width, local_blocks, tile_width)
    wanted = lax.all_to_all(requests, ("group", "peer"), split_axis=0, concat_axis=0, tiled=True)
    picked = jnp.maximum(wanted, 0).reshape(-1)
    served = jnp.take(advanced, picked, axis=1)
    arrived = lax.all_to_all(
        served.reshape(width, wanted.shape[0], wanted.shape[1], tile_width),
        ("group", "peer"),
        split_axis=1,
        concat_axis=1,
        tiled=True,
    )
    flat_cols = (slot_index[:, None] * tile_width + tile_perm).reshape(-1)
    return jnp.take(arrived.reshape(width, devices * capacity * tile_width), flat_cols, axis=1)


def solution(mesh):
    return jax.shard_map(
        on_device,
        mesh=mesh,
        in_specs=(
            P(None, ("group", "peer")),
            P(("group", "peer")),
            P(("group", "peer"), None),
            P(),
            P(),
            P(),
            P(),
            P(),
        ),
        out_specs=P(None, ("group", "peer")),
        check_vma=False,
    )
```

profile of v0, /device:TPU:25, one launch (start us, length us, event | category | flops | bytes accessed | tf_op | source)
XLA Modules:
  0.0 510.8 jit_solution(10718963295124107990)
XLA Ops:
  0.0 0.8 convert_reduce_fusion
  0.8 0.2 dynamic-update-slice
  1.0 38.3 %all-reduce = s32[1024]{0:T(1024)S(1)} all-reduce(s32[1024]{0:T(1024)S(1)} %dynamic-update-slice), channel_id=2, replica_groups=mesh['group'=4,'peer'=8] {'group','peer'}, use_global_device_ids=true, to_apply=%add | all-reduce | flops 1024 | bytes 8192
  39.3 0.1 reshape.141
  39.4 0.5 while.10
  39.9 0.7 fusion.2
  40.6 0.6 reduce-window.6
  41.2 0.2 slice_reduce_fusion
  41.4 0.8 select_reduce_fusion
  42.2 0.7 broadcast_multiply_fusion.1
  42.9 1.4 scatter_custom_fusion
  44.3 0.7 all_to_all.9
  45.0 7.2 %all-to-all-start = ((s32[32,1,16]{2,1,0:T(1,128)}), s32[32,1,16]{2,1,0:T(1,128)S(1)}, u32[]{:S(2)}, u32[]{:S(2)}) async-start(s32[32,1,16]{2,1,0:T(1,128)} %bitcast.4), calls=%async_computation | async-start | bytes 32768 | tf_op jit(solution)/shard_map/all_to_all | solution.py:58
  52.1 0.7 neg.11
  52.8 1.5 divide_add_fusion
  54.3 6.4 %multiply_reduce_fusion = (f32[32768]{0:T(1024)S(1)}, f32[40,32768]{1,0:T(8,128)S(1)}) fusion(f32[40]{0:T(128)} %param.17, f32[32768]{0:T(1024)S(1)} %bitcast.45, f32[40]{0:T(128)} %param.16, f32[32768]{0:T(1024)S(1)} %bitcast.44, f32[40]{0:T(128)S(1)} %neg.11, f32[41,32768]{1,0:T(8,128)} %param.10, f32[40]{0:T(128)} %param.14, f32[40]{0:T(128)} %param.13), kind=kLoop, calls=%fused_computation.7 | loop fusion | flops 17006592 | bytes 10879776 | tf_op jit(solution)/shard_map/reduce_sum | solution.py:26
  60.7 1.3 slice_subtract_fusion
  62.1 0.5 pad_maximum_fusion
  62.6 1.1 copy.34
  63.7 0.6 slice.21
  64.2 5.9 %copy.29 = f32[41,256,128]{2,0,1:T(8,128)} copy(f32[41,256,128]{2,1,0:T(8,128)S(1)} %slice.21) | data formatting | bytes 10747904 | tf_op jit(solution)/shard_map/reshape | solution.py:57
  70.1 0.0 all-to-all-done
  70.1 0.1 copy.26
  70.2 0.1 copy.27
  70.3 0.1 copy.28
  70.4 0.1 reshape.119
  70.5 8.7 %gather_fusion = f32[512,41,128]{2,1,0:T(8,128)} fusion(f32[41,256,128]{2,0,1:T(8,128)} %copy.29, s32[1024]{0:T(1024)S(1)} %pad_clamp_fusion), kind=kCustom, calls=%fused_computation | custom fusion | bytes 21497856 | tf_op jit(solution)/shard_map/jit(_take)/gather | solution.py:60
  79.2 14.1 %copy_select_fusion = f32[41,32,16,128]{3,2,0,1:T(8,128)} fusion(f32[41,32,16,128]{3,0,2,1:T(8,128)} %bitcast.41, pred[32,16]{1,0:T(8,128)(4,1)S(1)} %copy.27), kind=kLoop, calls=%fused_computation.5 | loop fusion | flops 2686976 | bytes 21496320 | tf_op jit(solution)/shard_map/jit(_take)/select_n | solution.py:60
  93.3 0.0 copy-start
  93.3 5.9 %all-to-all-start.1 = ((f32[41,32,16,128]{3,2,0,1:T(8,128)}), f32[41,32,16,128]{3,2,0,1:T(8,128)}, u32[]{:S(2)}, u32[]{:S(2)}) async-start(f32[41,32,16,128]{3,2,0,1:T(8,128)} %copy_select_fusion), calls=%async_computation.1 | async-start | bytes 21495808 | tf_op jit(solution)/shard_map/all_to_all | solution.py:61
  99.2 0.0 copy-done
  99.2 0.1 compare_and_fusion
  99.3 0.1 compare_select_fusion
  99.5 240.6 %all-to-all-done.1 = f32[41,32,16,128]{3,2,0,1:T(8,128)} async-done(((f32[41,32,16,128]{3,2,0,1:T(8,128)}), f32[41,32,16,128]{3,2,0,1:T(8,128)}, u32[]{:S(2)}, u32[]{:S(2)}) %all-to-all-start.1) | async-done | bytes 10747936 | tf_op jit(solution)/shard_map/all_to_all | solution.py:61
  340.0 20.7 %copy.31 = f32[41,32,16,128]{0,3,2,1:T(8,128)} copy(f32[41,32,16,128]{3,2,0,1:T(8,128)} %all-to-all-done.1) | data formatting | bytes 21495808 | tf_op jit(solution)/shard_map/all_to_all | solution.py:61
  360.8 118.8 %gather_fusion.1 = f32[32768,41]{1,0:T(8,128)} fusion(f32[41,65536]{0,1:T(8,128)} %bitcast.40, s32[32768]{0:T(1024)S(1)} %broadcast_clamp_fusion), kind=kCustom, calls=%fused_computation.1 | custom fusion | bytes 10878976 | tf_op jit(solution)/shard_map/jit(_take)/gather | solution.py:69
  479.6 19.1 %select_bitcast_fusion = f32[41,32768]{0,1:T(8,128)} fusion(f32[32768,41]{1,0:T(8,128)} %gather_fusion.1, pred[32768]{0:T(1024)(128)(4,1)S(1)} %get-tuple-element.39), kind=kLoop, calls=%fused_computation.4 | loop fusion | flops 1343488 | bytes 10780672 | tf_op jit(solution)/shard_map/jit(_take)/select_n | solution.py:69
  498.7 12.1 %copy.32 = f32[41,32768]{1,0:T(8,128)} copy(f32[41,32768]{0,1:T(8,128)} %select_bitcast_fusion) | data formatting | bytes 10747904 | tf_op jit(solution)/shard_map/jit(_take)/select_n | solution.py:69
  (23 shorter events, 0.3 us)
Async XLA Ops:
  45.0 25.2 %all-to-all-start = ((s32[32,1,16]{2,1,0:T(1,128)}), s32[32,1,16]{2,1,0:T(1,128)S(1)}, u32[]{:S(2)}, u32[]{:S(2)}) async-start(s32[32,1,16]{2,1,0:T(1,128)} %bitcast.4), calls=%async_computation | async-start | bytes 32768 | tf_op jit(solution)/shard_map/all_to_all | solution.py:58
  93.3 5.9 %copy-start = (s32[256,128]{1,0:T(8,128)S(1)}, s32[256,128]{1,0:T(8,128)}, u32[]{:S(2)}) copy-start(s32[256,128]{1,0:T(8,128)} %param.12) | copy-start | bytes 393220
  93.3 246.8 %all-to-all-start.1 = ((f32[41,32,16,128]{3,2,0,1:T(8,128)}), f32[41,32,16,128]{3,2,0,1:T(8,128)}, u32[]{:S(2)}, u32[]{:S(2)}) async-start(f32[41,32,16,128]{3,2,0,1:T(8,128)} %copy_select_fusion), calls=%async_computation.1 | async-start | bytes 21495808 | tf_op jit(solution)/shard_map/all_to_all | solution.py:61
where the time goes:
time: 512 us; the launch traced here: 511 us
  waiting for transfers between devices  241 us (47%)
  local copies, waits for them, and re-layouts  171 us (33%)
  other arithmetic  47.6 us (9%)
  blocking collectives  38.3 us (7%)
  starting transfers between devices  13 us (3%)
    all_to_all x1, waiting for transfers between devices, on_device(): lax.all_to_all(served.reshape(width, wanted.shape[0], wanted.shape[1], ti...  241 us
    gather x1, local copies, waits for them, and re-layouts, on_device(): jnp.take(arrived.reshape(width, devices * capacity * tile_width), flat_co...  119 us
    unnamed x1, blocking collectives  38.3 us
    all_to_all x1, local copies, waits for them, and re-layouts, on_device(): lax.all_to_all(served.reshape(width, wanted.shape[0], wanted.shape[1], ti...  20.7 us
    select_n x2, other arithmetic, on_device(): jnp.take(arrived.reshape(width, devices * capacity * tile_width), flat_co...  19.2 us
    select_n x1, other arithmetic, on_device(): served = jnp.take(advanced, picked, axis=1)  14.1 us
    select_n x1, local copies, waits for them, and re-layouts, on_device(): jnp.take(arrived.reshape(width, devices * capacity * tile_width), flat_co...  12.1 us
  transfers between devices with their start and end apart: 2, of which 1 were waited for; matrix products, arithmetic and copies ran while one was open for 4% of the time, Pallas kernels for 0%

commit v1 on v0

--- a/solution.py
+++ b/solution.py
@@ -58,12 +58,21 @@
     wanted = lax.all_to_all(requests, ("group", "peer"), split_axis=0, concat_axis=0, tiled=True)
     picked = jnp.maximum(wanted, 0).reshape(-1)
     served = jnp.take(advanced, picked, axis=1)
-    arrived = lax.all_to_all(
-        served.reshape(width, wanted.shape[0], wanted.shape[1], tile_width),
-        ("group", "peer"),
-        split_axis=1,
-        concat_axis=1,
-        tiled=True,
+    arrived = jnp.concatenate(
+        jax.lax.all_to_all(
+            jnp.stack(
+                jnp.split(
+                    served.reshape(width, wanted.shape[0], wanted.shape[1], tile_width),
+                    jax.lax.axis_size(("group", "peer")),
+                    1,
+                ),
+                axis=0,
+            ),
+            axis_name=("group", "peer"),
+            split_axis=0,
+            concat_axis=0,
+        ),
+        1,
     )
     flat_cols = (slot_index[:, None] * tile_width + tile_perm).reshape(-1)
     return jnp.take(arrived.reshape(width, devices * capacity * tile_width), flat_cols, axis=1)

time: 512 us -> 568 us (1.11)
  local copies, waits for them, and re-layouts: 171 us -> 226 us
    unnamed x5 -> x36, local copies, waits for them, and re-layouts: 1.33 us -> 55 us
    all_to_all x1 -> x0, local copies, waits for them, and re-layouts: 20.7 us -> none  [on_device(): lax.all_to_all(served.reshape(width, wanted.shape[0], wanted.shape[1], ti...]
    reshape x0 -> x1, local copies, waits for them, and re-layouts: none -> 20.7 us  [on_device(): jnp.concatenate(jax.lax.all_to_all(jnp.stack(jnp.split(served.reshape(wid...]
  transfers between devices with their start and end apart: 2 -> 2, of which waited for: 1 -> 1; matrix products, arithmetic and copies ran while one was open for 4% -> 3% of each run, Pallas kernels for 0% -> 0%
where the time goes in v1:
time: 568 us; the launch traced here: 566 us
  waiting for transfers between devices  241 us (42%)
  local copies, waits for them, and re-layouts  226 us (40%)
  other arithmetic  47.6 us (8%)
  blocking collectives  38.3 us (7%)
  starting transfers between devices  13 us (2%)
    all_to_all x1, waiting for transfers between devices, on_device(): jax.lax.all_to_all(jnp.stack(jnp.split(served.reshape(width, wanted.shape...  241 us
    gather x1, local copies, waits for them, and re-layouts, on_device(): jnp.take(arrived.reshape(width, devices * capacity * tile_width), flat_co...  119 us
    unnamed x36, local copies, waits for them, and re-layouts  55 us
    unnamed x1, blocking collectives  38.3 us
    reshape x1, local copies, waits for them, and re-layouts, on_device(): jnp.concatenate(jax.lax.all_to_all(jnp.stack(jnp.split(served.reshape(wid...  20.7 us
    select_n x2, other arithmetic, on_device(): jnp.take(arrived.reshape(width, devices * capacity * tile_width), flat_co...  19.2 us
    select_n x1, other arithmetic, on_device(): served = jnp.take(advanced, picked, axis=1)  14.1 us
    select_n x1, local copies, waits for them, and re-layouts, on_device(): jnp.take(arrived.reshape(width, devices * capacity * tile_width), flat_co...  12.1 us
  transfers between devices with their start and end apart: 2, of which 1 were waited for; matrix products, arithmetic and copies ran while one was open for 3% of the time, Pallas kernels for 0%

profile of v1, /device:TPU:25, one launch (start us, length us, event | category | flops | bytes accessed | tf_op | source)
XLA Modules:
  0.0 566.2 jit_solution(7285395196520501991)
XLA Ops:
  1.0 38.3 %all-reduce = s32[1024]{0:T(1024)S(1)} all-reduce(s32[1024]{0:T(1024)S(1)} %dynamic-update-slice), channel_id=2, replica_groups=mesh['group'=4,'peer'=8] {'group','peer'}, use_global_device_ids=true, to_apply=%add | all-reduce | flops 1024 | bytes 8192
  42.9 1.4 scatter_custom_fusion
  45.0 7.2 %all-to-all-start = ((s32[32,1,16]{2,1,0:T(1,128)}), s32[32,1,16]{2,1,0:T(1,128)S(1)}, u32[]{:S(2)}, u32[]{:S(2)}) async-start(s32[32,1,16]{2,1,0:T(1,128)} %bitcast.4), calls=%async_computation | async-start | bytes 32768 | tf_op jit(solution)/shard_map/all_to_all | solution.py:58
  52.8 1.5 divide_add_fusion
  54.3 6.4 %multiply_reduce_fusion = (f32[32768]{0:T(1024)S(1)}, f32[40,32768]{1,0:T(8,128)S(1)}) fusion(f32[40]{0:T(128)} %param.17, f32[32768]{0:T(1024)S(1)} %bitcast.236, f32[40]{0:T(128)} %param.16, f32[32768]{0:T(1024)S(1)} %bitcast.235, f32[40]{0:T(128)S(1)} %neg.11, f32[41,32768]{1,0:T(8,128)} %param.10, f32[40]{0:T(128)} %param.14, f32[40]{0:T(128)} %param.13), kind=kLoop, calls=%fused_computation.7 | loop fusion | flops 17006592 | bytes 10879776 | tf_op jit(solution)/shard_map/reduce_sum | solution.py:26
  60.7 1.3 slice_subtract_fusion
  62.6 1.1 copy.127
  64.2 5.9 %copy.91 = f32[41,256,128]{2,0,1:T(8,128)} copy(f32[41,256,128]{2,1,0:T(8,128)S(1)} %slice.21) | data formatting | bytes 10747904 | tf_op jit(solution)/shard_map/reshape | solution.py:57
  70.5 8.7 %gather_fusion = f32[512,41,128]{2,1,0:T(8,128)} fusion(f32[41,256,128]{2,0,1:T(8,128)} %copy.91, s32[1024]{0:T(1024)S(1)} %pad_clamp_fusion), kind=kCustom, calls=%fused_computation | custom fusion | bytes 21497856 | tf_op jit(solution)/shard_map/jit(_take)/gather | solution.py:60
  79.2 14.1 %copy_select_fusion = f32[41,32,16,128]{3,2,0,1:T(8,128)} fusion(f32[41,32,16,128]{3,0,2,1:T(8,128)} %bitcast.232, pred[32,16]{1,0:T(8,128)(4,1)S(1)} %copy.89), kind=kLoop, calls=%fused_computation.5 | loop fusion | flops 2686976 | bytes 21496320 | tf_op jit(solution)/shard_map/jit(_take)/select_n | solution.py:60
  93.3 1.7 fusion.31
  95.0 1.7 fusion.30
  96.7 1.7 fusion.29
  98.4 1.7 fusion.28
  100.2 1.7 fusion.27
  101.9 1.7 fusion.26
  103.6 1.7 fusion.25
  105.4 1.7 fusion.24
  107.1 1.7 fusion.23
  108.8 1.8 fusion.22
  110.6 1.7 fusion.21
  112.3 1.7 fusion.20
  114.0 1.7 fusion.19
  115.7 1.7 fusion.18
  117.5 1.7 fusion.17
  119.2 1.7 fusion.16
  120.9 1.7 fusion.15
  122.7 1.7 fusion.14
  124.4 1.7 fusion.13
  126.1 1.7 fusion.12
  127.9 1.7 fusion.11
  129.6 1.7 fusion.10
  131.3 1.7 fusion.9
  133.0 1.7 fusion.8
  134.8 1.7 fusion.7
  136.5 1.7 fusion.6
  138.2 1.7 fusion.5
  140.0 1.8 fusion.4
  141.7 1.7 fusion.3
  143.5 1.7 fusion.2
  145.2 1.7 fusion.1
  146.9 1.8 fusion
  148.7 5.9 %all-to-all-start.1 = ((f32[32,41,1,16,128]{4,3,2,1,0:T(8,128)}), f32[32,41,1,16,128]{4,3,2,1,0:T(8,128)}, u32[]{:S(2)}, u32[]{:S(2)}) async-start(f32[32,41,1,16,128]{4,3,2,1,0:T(8,128)} %fusion), calls=%async_computation.1 | async-start | bytes 21495808 | tf_op jit(solution)/shard_map/all_to_all | solution.py:62
  154.9 240.6 %all-to-all-done.1 = f32[32,41,1,16,128]{4,3,2,1,0:T(8,128)} async-done(((f32[32,41,1,16,128]{4,3,2,1,0:T(8,128)}), f32[32,41,1,16,128]{4,3,2,1,0:T(8,128)}, u32[]{:S(2)}, u32[]{:S(2)}) %all-to-all-start.1) | async-done | bytes 10747936 | tf_op jit(solution)/shard_map/all_to_all | solution.py:62
  395.5 20.7 %copy.124 = f32[41,32,1,16,128]{0,4,3,1,2:T(8,128)} copy(f32[41,32,1,16,128]{4,3,2,0,1:T(8,128)} %bitcast.74) | data formatting | bytes 21495808 | tf_op jit(solution)/shard_map/reshape | solution.py:61
  416.2 118.8 %gather_fusion.1 = f32[32768,41]{1,0:T(8,128)} fusion(f32[41,65536]{0,1:T(8,128)} %bitcast.231, s32[32768]{0:T(1024)S(1)} %broadcast_clamp_fusion), kind=kCustom, calls=%fused_computation.1 | custom fusion | bytes 10878976 | tf_op jit(solution)/shard_map/jit(_take)/gather | solution.py:78
  535.0 19.1 %select_bitcast_fusion = f32[41,32768]{0,1:T(8,128)} fusion(f32[32768,41]{1,0:T(8,128)} %gather_fusion.1, pred[32768]{0:T(1024)(128)(4,1)S(1)} %get-tuple-element.39), kind=kLoop, calls=%fused_computation.4 | loop fusion | flops 1343488 | bytes 10780672 | tf_op jit(solution)/shard_map/jit(_take)/select_n | solution.py:78
  554.1 12.1 %copy.125 = f32[41,32768]{1,0:T(8,128)} copy(f32[41,32768]{0,1:T(8,128)} %select_bitcast_fusion) | data formatting | bytes 10747904 | tf_op jit(solution)/shard_map/jit(_take)/select_n | solution.py:78
  (45 shorter events, 7.8 us)
Async XLA Ops:
  45.0 25.2 %all-to-all-start = ((s32[32,1,16]{2,1,0:T(1,128)}), s32[32,1,16]{2,1,0:T(1,128)S(1)}, u32[]{:S(2)}, u32[]{:S(2)}) async-start(s32[32,1,16]{2,1,0:T(1,128)} %bitcast.4), calls=%async_computation | async-start | bytes 32768 | tf_op jit(solution)/shard_map/all_to_all | solution.py:58
  148.7 5.9 %copy-start = (s32[256,128]{1,0:T(8,128)S(1)}, s32[256,128]{1,0:T(8,128)}, u32[]{:S(2)}) copy-start(s32[256,128]{1,0:T(8,128)} %param.12) | copy-start | bytes 393220
  148.7 246.8 %all-to-all-start.1 = ((f32[32,41,1,16,128]{4,3,2,1,0:T(8,128)}), f32[32,41,1,16,128]{4,3,2,1,0:T(8,128)}, u32[]{:S(2)}, u32[]{:S(2)}) async-start(f32[32,41,1,16,128]{4,3,2,1,0:T(8,128)} %fusion), calls=%async_computation.1 | async-start | bytes 21495808 | tf_op jit(solution)/shard_map/all_to_all | solution.py:62
